TPU v7x, 32 devices: a whole 2x2x4 slice. The times are simulated.
32 devices in a mesh: fsdp: 2 (over core), width: 4 (over y, x), unit: 4 (over z).
Axes of the slice: x: 2, y: 2, z: 4, core: 2. Of those that a mesh axis runs over, the one named last changes fastest.
Arguments:
- train_gate: bfloat16 [8192, 8192], P(('unit', 'fsdp'), 'width'), parts along dimension 0, may hold values from -0.125 to 0.125
- low_gate: bfloat16 [8192, 32], P(('unit', 'fsdp')), parts along dimension 0, may hold values from -0.125 to 0.125
- high_gate: bfloat16 [128, 8192], P('unit', 'width'), parts along dimension 0, may hold values from -1 to 1
- train_up: bfloat16 [8192, 8192], P(('unit', 'fsdp'), 'width'), parts along dimension 0, may hold values from -0.125 to 0.125
- low_up: bfloat16 [8192, 32], P(('unit', 'fsdp')), parts along dimension 0, may hold values from -0.125 to 0.125
- high_up: bfloat16 [128, 8192], P('unit', 'width'), parts along dimension 0, may hold values from -1 to 1
- norm_train: float32 [8192], P(('unit', 'fsdp', 'width')), parts along dimension 0, may hold values from 0.25 to 1.75
- norm_step: float32 [8192], P(('unit', 'fsdp', 'width')), parts along dimension 0, may hold values from -0.3 to 0.3
Outputs:
- final_gate: bfloat16 [32768, 2048], P(('unit', 'width')), parts along dimension 0
- final_up: bfloat16 [32768, 2048], P(('unit', 'width')), parts along dimension 0
- serve_norm: bfloat16 [8192], P('unit'), parts along dimension 0
There are 4 independent parts, one for each index of `unit`. A program takes and returns all parts, laid end to end along the dimension named above; each array names one. Nothing has to cross between parts.
All inputs are finite; a program needn't handle non-finite values.
Results may differ from a plain program's by a relative error of at most 0.001.
Values may be sent and summed in bfloat16 or wider, within the bound.
A program may use at most 128 MiB of HBM per device.

v0:
```python
import jax
import jax.numpy as jnp
from jax import lax
from jax.sharding import PartitionSpec as P

mix_rate = 2.0


def body(train_gate, low_gate, high_gate, train_up, low_up, high_up, norm_train, norm_step):
    result_gate = train_gate.astype(jnp.float32) + mix_rate * jnp.dot(
        low_gate, high_gate, preferred_element_type=jnp.float32
    )
    result_up = train_up.astype(jnp.float32) + mix_rate * jnp.dot(
        low_up, high_up, preferred_element_type=jnp.float32
    )
    narrow_gate, narrow_up = (result_gate.astype(jnp.bfloat16), result_up.astype(jnp.bfloat16))
    final_gate, final_up = (
        lax.all_gather(narrow_gate, "fsdp", axis=0, tiled=True),
        lax.all_gather(narrow_up, "fsdp", axis=0, tiled=True),
    )
    final_gate, final_up = (final_gate.T, final_up.T)
    serve_norm = lax.all_gather(
        (norm_train + norm_step).astype(jnp.bfloat16), ("fsdp", "width"), axis=0, tiled=True
    )
    return (final_gate, final_up, serve_norm)


def solution(mesh):
    return jax.shard_map(
        body,
        mesh=mesh,
        in_specs=(
            P(("unit", "fsdp"), "width"),
            P(("unit", "fsdp"), None),
            P("unit", "width"),
            P(("unit", "fsdp"), "width"),
            P(("unit", "fsdp"), None),
            P("unit", "width"),
            P(("unit", "fsdp", "width")),
            P(("unit", "fsdp", "width")),
        ),
        out_specs=(P(("unit", "width"), None), P(("unit", "width"), None), P("unit")),
        check_vma=False,
    )
```

profile of v0, /device:TPU:0, one launch (start us, length us, event | category | flops | bytes accessed | tf_op | source)
XLA Modules:
  0.0 78.0 jit_solution(2958209487717878340)
XLA Ops:
  7.2 0.0 copy-start
  7.2 0.0 copy-start.2
  7.2 0.0 copy-start.1
  7.2 0.0 all-gather.4.cloned.1.call-start
  7.2 0.8 %copy-done = bf16[32,2048]{1,0:T(8,128)(2,1)S(1)} copy-done((bf16[32,2048]{1,0:T(8,128)(2,1)S(1)}, bf16[32,2048]{1,0:T(8,128)(2,1)}, u32[]{:S(2)}) %copy-start) | copy-done | bytes 131096
  8.1 5.5 %add_convert_fusion.1 = bf16[1024,2048]{1,0:T(8,128)(2,1)} fusion(bf16[1024,2048]{1,0:T(8,128)(2,1)} %param.8, bf16[1024,32]{0,1:T(8,128)(2,1)} %param.9, bf16[32,2048]{1,0:T(8,128)(2,1)S(1)} %copy-done), kind=kOutput, calls=%fused_computation.1 | convolution fusion | flops 142606336 | bytes 8585216 | tf_op jit(solution)/shard_map/dot_general | solution.py:10
  13.6 0.0 copy-start.3
  13.6 0.0 copy-start.4
  13.6 0.0 all-gather.4.cloned.1.call-update
  13.6 0.0 all-gather.6.cloned.1.call-start
  13.7 0.0 copy-done.2
  13.7 0.0 copy-done.1
  13.7 5.4 %add_convert_fusion = bf16[1024,2048]{1,0:T(8,128)(2,1)} fusion(bf16[1024,2048]{1,0:T(8,128)(2,1)} %param.11, bf16[1024,32]{0,1:T(8,128)(2,1)S(1)} %copy-done.2, bf16[32,2048]{1,0:T(8,128)(2,1)S(1)} %copy-done.1), kind=kOutput, calls=%fused_computation | convolution fusion | flops 142606336 | bytes 8585216 | tf_op jit(solution)/shard_map/dot_general | solution.py:13
  19.1 0.0 all-gather.6.cloned.1.call-update
  19.1 0.0 copy-done.3
  19.1 0.0 copy-done.4
  19.2 14.9 %all-gather = bf16[8,1,256]{2,1,0:T(2,128)(2,1)S(1)} all-gather(bf16[1,1,256]{2,1,0:T(2,128)(2,1)S(1)} %reshape.6), channel_id=1, replica_groups=mesh['fsdp'=2,'width'=4,'unit'=4] {'fsdp','width'}, dimensions={0}, use_global_device_ids=true | all-gather | bytes 4608 | tf_op jit(solution)/shard_map/all_gather | solution.py:22
  34.1 0.6 copy.17
  34.7 1.7 %all-gather.4.cloned.1.call-done = bf16[2048,2048]{1,0:T(8,128)(2,1)} async-done(((bf16[1024,2048]{1,0:T(8,128)(2,1)}), bf16[2048,2048]{1,0:T(8,128)(2,1)}) %all-gather.4.cloned.1.call-update) | async-done | bytes 8388624 | tf_op jit(solution)/shard_map/all_gather | solution.py:18
  36.4 12.3 %copy.15 = bf16[2048,2048]{1,0:T(8,128)(2,1)} copy(bf16[2048,2048]{0,1:T(8,128)(2,1)} %bitcast.8) | data formatting | bytes 16777216
  48.7 10.3 %all-gather.6.cloned.1.call-done = bf16[2048,2048]{1,0:T(8,128)(2,1)} async-done(((bf16[1024,2048]{1,0:T(8,128)(2,1)}), bf16[2048,2048]{1,0:T(8,128)(2,1)}) %all-gather.6.cloned.1.call-update) | async-done | bytes 8388624 | tf_op jit(solution)/shard_map/all_gather | solution.py:19
  58.9 12.2 %copy.16 = bf16[2048,2048]{1,0:T(8,128)(2,1)} copy(bf16[2048,2048]{0,1:T(8,128)(2,1)} %bitcast.9) | data formatting | bytes 16777216
  (3 shorter events, 0.0 us)
Async XLA Ops:
  7.2 0.9 %copy-start = (bf16[32,2048]{1,0:T(8,128)(2,1)S(1)}, bf16[32,2048]{1,0:T(8,128)(2,1)}, u32[]{:S(2)}) copy-start(bf16[32,2048]{1,0:T(8,128)(2,1)} %param.10) | copy-start | bytes 393220
  7.2 6.5 %copy-start.2 = (bf16[1024,32]{0,1:T(8,128)(2,1)S(1)}, bf16[1024,32]{0,1:T(8,128)(2,1)}, u32[]{:S(2)}) copy-start(bf16[1024,32]{0,1:T(8,128)(2,1)} %param.12) | copy-start | bytes 196612
  7.2 6.5 %copy-start.1 = (bf16[32,2048]{1,0:T(8,128)(2,1)S(1)}, bf16[32,2048]{1,0:T(8,128)(2,1)}, u32[]{:S(2)}) copy-start(bf16[32,2048]{1,0:T(8,128)(2,1)} %param.13) | copy-start | bytes 393220
  7.2 29.1 %all-gather.4.cloned.1.call-start = ((), (), s32[]{:S(2)}) async-start(), calls=%async_computation | async-start | bytes 12582912 | tf_op jit(solution)/shard_map/all_gather | solution.py:18
  13.6 5.5 %copy-start.3 = (f32[256]{0:T(256)S(1)}, f32[256]{0:T(256)}, u32[]{:S(2)}) copy-start(f32[256]{0:T(256)} %param.14) | copy-start | bytes 3076
  13.6 5.5 %copy-start.4 = (f32[256]{0:T(256)S(1)}, f32[256]{0:T(256)}, u32[]{:S(2)}) copy-start(f32[256]{0:T(256)} %param.15) | copy-start | bytes 3076
  13.6 45.3 %all-gather.6.cloned.1.call-start = ((), (), s32[]{:S(2)}) async-start(), calls=%async_computation.1 | async-start | bytes 12582912 | tf_op jit(solution)/shard_map/all_gather | solution.py:19
Sparse Core Ops, SparseCore 0:
  13.7 22.5 all-gather.3
  37.9 21.0 all-gather.5
where the time goes:
time: 78.8 us; the launch traced here: 78 us
  local copies, waits for them, and re-layouts  26 us (33%)
  blocking collectives  14.9 us (19%)
  between operations  14.1 us (18%)
  waiting for transfers between devices  12 us (15%)
  matrix products  10.9 us (14%)
    unnamed x14, local copies, waits for them, and re-layouts  26 us
    all_gather x1, blocking collectives, body(): lax.all_gather((norm_train + norm_step).astype(jnp.bfloat16), ('fsdp', 'w...  14.9 us
    all_gather x1, waiting for transfers between devices, body(): lax.all_gather(narrow_up, 'fsdp', axis=0, tiled=True)  10.3 us
    dot_general x1, matrix products, body(): jnp.dot(low_gate, high_gate, preferred_element_type=jnp.float32)  5.52 us
    dot_general x1, matrix products, body(): jnp.dot(low_up, high_up, preferred_element_type=jnp.float32)  5.41 us
    all_gather x1, waiting for transfers between devices, body(): lax.all_gather(narrow_gate, 'fsdp', axis=0, tiled=True)  1.67 us
  transfers between devices with their start and end apart: 2, of which 2 were waited for; matrix products, arithmetic and copies ran while one was open for 24% of the time, Pallas kernels for 0%

commit v1 on v0

--- a/solution.py
+++ b/solution.py
@@ -4,6 +4,18 @@
 from jax.sharding import PartitionSpec as P
 
 mix_rate = 2.0
+
+
+def collect(array, axis, dim):
+    ways, here = (lax.axis_size(axis), lax.axis_index(axis))
+    grown, reach = (array, 1)
+    while reach < ways:
+        theirs = lax.ppermute(grown, axis, [(d, d ^ reach) for d in range(ways)])
+        mine_first = jnp.concatenate([grown, theirs], axis=dim)
+        theirs_first = jnp.concatenate([theirs, grown], axis=dim)
+        grown = jnp.where(here & reach == 0, mine_first, theirs_first)
+        reach = 2 * reach
+    return grown
 
 
 def body(train_gate, low_gate, high_gate, train_up, low_up, high_up, norm_train, norm_step):
@@ -19,9 +31,7 @@
         lax.all_gather(narrow_up, "fsdp", axis=0, tiled=True),
     )
     final_gate, final_up = (final_gate.T, final_up.T)
-    serve_norm = lax.all_gather(
-        (norm_train + norm_step).astype(jnp.bfloat16), ("fsdp", "width"), axis=0, tiled=True
-    )
+    serve_norm = collect((norm_train + norm_step).astype(jnp.bfloat16), ("fsdp", "width"), 0)
     return (final_gate, final_up, serve_norm)
 
 

time: 78.8 us -> 78.8 us (level)
  blocking collectives: 14.9 us -> 0 us
  waiting for transfers between devices: 12 us -> 21.7 us
  starting transfers between devices: 0.08 us -> 5.28 us
    all_gather x1 -> x0, blocking collectives: 14.9 us -> none  [body(): lax.all_gather((norm_train + norm_step).astype(jnp.bfloat16), ('fsdp', 'w...]
    all_gather x1, waiting for transfers between devices: 1.67 us -> 7.11 us  [body(): lax.all_gather(narrow_gate, 'fsdp', axis=0, tiled=True)]
    ppermute x0 -> x3, starting transfers between devices: none -> 5.2 us  [collect(): theirs = lax.ppermute(grown, axis, [(d, d ^ reach) for d in range(ways)])]
    ppermute x0 -> x3, waiting for transfers between devices: none -> 4.25 us  [collect(): theirs = lax.ppermute(grown, axis, [(d, d ^ reach) for d in range(ways)])]
    unnamed x14 -> x12, local copies, waits for them, and re-layouts: 26 us -> 25.4 us
  transfers between devices with their start and end apart: 2 -> 5, of which waited for: 2 -> 5; matrix products, arithmetic and copies ran while one was open for 24% -> 24% of each run, Pallas kernels for 0% -> 0%
where the time goes in v1:
time: 78.8 us; the launch traced here: 78 us
  local copies, waits for them, and re-layouts  25.4 us (32%)
  waiting for transfers between devices  21.7 us (28%)
  between operations  14.1 us (18%)
  matrix products  10.9 us (14%)
  starting transfers between devices  5.28 us (7%)
    unnamed x12, local copies, waits for them, and re-layouts  25.4 us
    all_gather x1, waiting for transfers between devices, body(): lax.all_gather(narrow_up, 'fsdp', axis=0, tiled=True)  10.3 us
    all_gather x1, waiting for transfers between devices, body(): lax.all_gather(narrow_gate, 'fsdp', axis=0, tiled=True)  7.11 us
    dot_general x1, matrix products, body(): jnp.dot(low_gate, high_gate, preferred_element_type=jnp.float32)  5.52 us
    dot_general x1, matrix products, body(): jnp.dot(low_up, high_up, preferred_element_type=jnp.float32)  5.41 us
    ppermute x3, starting transfers between devices, collect(): theirs = lax.ppermute(grown, axis, [(d, d ^ reach) for d in range(ways)])  5.2 us
    ppermute x3, waiting for transfers between devices, collect(): theirs = lax.ppermute(grown, axis, [(d, d ^ reach) for d in range(ways)])  4.25 us
  transfers between devices with their start and end apart: 5, of which 5 were waited for; matrix products, arithmetic and copies ran while one was open for 24% of the time, Pallas kernels for 0%

profile of v1, /device:TPU:0, one launch (start us, length us, event | category | flops | bytes accessed | tf_op | source)
XLA Modules:
  0.0 78.0 jit_solution(7873092715766185569)
XLA Ops:
  7.2 0.0 copy-start
  7.2 0.0 copy-start.2
  7.2 0.0 copy-start.1
  7.2 0.0 all-gather.3.cloned.1.call-start
  7.2 0.8 %copy-done = bf16[32,2048]{1,0:T(8,128)(2,1)S(1)} copy-done((bf16[32,2048]{1,0:T(8,128)(2,1)S(1)}, bf16[32,2048]{1,0:T(8,128)(2,1)}, u32[]{:S(2)}) %copy-start) | copy-done | bytes 131096
  8.1 5.5 %add_convert_fusion.1 = bf16[1024,2048]{1,0:T(8,128)(2,1)} fusion(bf16[1024,2048]{1,0:T(8,128)(2,1)} %param.8, bf16[1024,32]{0,1:T(8,128)(2,1)} %param.9, bf16[32,2048]{1,0:T(8,128)(2,1)S(1)} %copy-done), kind=kOutput, calls=%fused_computation.1 | convolution fusion | flops 142606336 | bytes 8585216 | tf_op jit(solution)/shard_map/dot_general | solution.py:22
  13.6 0.0 copy-start.3
  13.6 0.0 copy-start.4
  13.6 0.0 all-gather.3.cloned.1.call-update
  13.6 0.0 all-gather.5.cloned.1.call-start
  13.7 0.0 copy-done.2
  13.7 0.0 copy-done.1
  13.7 5.4 %add_convert_fusion = bf16[1024,2048]{1,0:T(8,128)(2,1)} fusion(bf16[1024,2048]{1,0:T(8,128)(2,1)} %param.11, bf16[1024,32]{0,1:T(8,128)(2,1)S(1)} %copy-done.2, bf16[32,2048]{1,0:T(8,128)(2,1)S(1)} %copy-done.1), kind=kOutput, calls=%fused_computation | convolution fusion | flops 142606336 | bytes 8585216 | tf_op jit(solution)/shard_map/dot_general | solution.py:25
  19.1 0.0 all-gather.5.cloned.1.call-update
  19.1 0.0 copy-done.3
  19.1 0.0 copy-done.4
  19.2 3.0 %collective-permute-start = (bf16[256]{0:T(256)(128)(2,1)S(1)}, bf16[256]{0:T(256)(128)(2,1)S(1)}, u32[]{:S(2)}, u32[]{:S(2)}) collective-permute-start(bf16[256]{0:T(256)(128)(2,1)S(1)} %add_convert_fusion.2), channel_id=1, source_target_pairs={{0,4},{4,0},{8,12},{12,8},{16,20},{20,16},{24,28},{28,24},{1,5},{5... | collective-permute-start | bytes 1544 | tf_op jit(solution)/shard_map/ppermute | solution.py:13
  22.2 1.5 %collective-permute-done = bf16[256]{0:T(256)(128)(2,1)S(1)} collective-permute-done((bf16[256]{0:T(256)(128)(2,1)S(1)}, bf16[256]{0:T(256)(128)(2,1)S(1)}, u32[]{:S(2)}, u32[]{:S(2)}) %collective-permute-start) | collective-permute-done | bytes 544 | tf_op jit(solution)/shard_map/ppermute | solution.py:13
  23.8 2.1 %collective-permute-start.1 = (bf16[512]{0:T(512)(128)(2,1)S(1)}, bf16[512]{0:T(512)(128)(2,1)S(1)}, u32[]{:S(2)}, u32[]{:S(2)}) collective-permute-start(bf16[512]{0:T(512)(128)(2,1)S(1)} %maximum_select_fusion.2), channel_id=1, source_target_pairs={{0,8},{4,12},{8,0},{12,4},{16,24},{20,28},{24,16},{28,20},{1,9},{5... | collective-permute-start | bytes 3080 | tf_op jit(solution)/shard_map/ppermute | solution.py:13
  25.9 1.6 %collective-permute-done.1 = bf16[512]{0:T(512)(128)(2,1)S(1)} collective-permute-done((bf16[512]{0:T(512)(128)(2,1)S(1)}, bf16[512]{0:T(512)(128)(2,1)S(1)}, u32[]{:S(2)}, u32[]{:S(2)}) %collective-permute-start.1) | collective-permute-done | bytes 1056 | tf_op jit(solution)/shard_map/ppermute | solution.py:13
  27.4 0.1 collective-permute-start.2
  27.5 1.1 %collective-permute-done.2 = bf16[1024]{0:T(1024)(128)(2,1)S(1)} collective-permute-done((bf16[1024]{0:T(1024)(128)(2,1)S(1)}, bf16[1024]{0:T(1024)(128)(2,1)S(1)}, u32[]{:S(2)}, u32[]{:S(2)}) %collective-permute-start.2) | collective-permute-done | bytes 2080 | tf_op jit(solution)/shard_map/ppermute | solution.py:13
  28.6 0.6 maximum_select_fusion
  29.2 7.1 %all-gather.3.cloned.1.call-done = bf16[2048,2048]{1,0:T(8,128)(2,1)} async-done(((bf16[1024,2048]{1,0:T(8,128)(2,1)}), bf16[2048,2048]{1,0:T(8,128)(2,1)}) %all-gather.3.cloned.1.call-update) | async-done | bytes 8388624 | tf_op jit(solution)/shard_map/all_gather | solution.py:30
  36.4 12.3 %copy.11 = bf16[2048,2048]{1,0:T(8,128)(2,1)} copy(bf16[2048,2048]{0,1:T(8,128)(2,1)} %bitcast.6) | data formatting | bytes 16777216
  48.7 10.3 %all-gather.5.cloned.1.call-done = bf16[2048,2048]{1,0:T(8,128)(2,1)} async-done(((bf16[1024,2048]{1,0:T(8,128)(2,1)}), bf16[2048,2048]{1,0:T(8,128)(2,1)}) %all-gather.5.cloned.1.call-update) | async-done | bytes 8388624 | tf_op jit(solution)/shard_map/all_gather | solution.py:31
  58.9 12.2 %copy.12 = bf16[2048,2048]{1,0:T(8,128)(2,1)} copy(bf16[2048,2048]{0,1:T(8,128)(2,1)} %bitcast.7) | data formatting | bytes 16777216
  (3 shorter events, 0.0 us)
Async XLA Ops:
  7.2 0.9 %copy-start = (bf16[32,2048]{1,0:T(8,128)(2,1)S(1)}, bf16[32,2048]{1,0:T(8,128)(2,1)}, u32[]{:S(2)}) copy-start(bf16[32,2048]{1,0:T(8,128)(2,1)} %param.10) | copy-start | bytes 393220
  7.2 6.5 %copy-start.2 = (bf16[1024,32]{0,1:T(8,128)(2,1)S(1)}, bf16[1024,32]{0,1:T(8,128)(2,1)}, u32[]{:S(2)}) copy-start(bf16[1024,32]{0,1:T(8,128)(2,1)} %param.12) | copy-start | bytes 196612
  7.2 6.5 %copy-start.1 = (bf16[32,2048]{1,0:T(8,128)(2,1)S(1)}, bf16[32,2048]{1,0:T(8,128)(2,1)}, u32[]{:S(2)}) copy-start(bf16[32,2048]{1,0:T(8,128)(2,1)} %param.13) | copy-start | bytes 393220
  7.2 29.1 %all-gather.3.cloned.1.call-start = ((), (), s32[]{:S(2)}) async-start(), calls=%async_computation | async-start | bytes 12582912 | tf_op jit(solution)/shard_map/all_gather | solution.py:30
  13.6 5.5 %copy-start.3 = (f32[256]{0:T(256)S(1)}, f32[256]{0:T(256)}, u32[]{:S(2)}) copy-start(f32[256]{0:T(256)} %param.14) | copy-start | bytes 3076
  13.6 5.5 %copy-start.4 = (f32[256]{0:T(256)S(1)}, f32[256]{0:T(256)}, u32[]{:S(2)}) copy-start(f32[256]{0:T(256)} %param.15) | copy-start | bytes 3076
  13.6 45.3 %all-gather.5.cloned.1.call-start = ((), (), s32[]{:S(2)}) async-start(), calls=%async_computation.1 | async-start | bytes 12582912 | tf_op jit(solution)/shard_map/all_gather | solution.py:31
  19.2 4.6 %collective-permute-start = (bf16[256]{0:T(256)(128)(2,1)S(1)}, bf16[256]{0:T(256)(128)(2,1)S(1)}, u32[]{:S(2)}, u32[]{:S(2)}) collective-permute-start(bf16[256]{0:T(256)(128)(2,1)S(1)} %add_convert_fusion.2), channel_id=1, source_target_pairs={{0,4},{4,0},{8,12},{12,8},{16,20},{20,16},{24,28},{28,24},{1,5},{5... | collective-permute-start | bytes 1544 | tf_op jit(solution)/shard_map/ppermute | solution.py:13
  23.8 3.7 %collective-permute-start.1 = (bf16[512]{0:T(512)(128)(2,1)S(1)}, bf16[512]{0:T(512)(128)(2,1)S(1)}, u32[]{:S(2)}, u32[]{:S(2)}) collective-permute-start(bf16[512]{0:T(512)(128)(2,1)S(1)} %maximum_select_fusion.2), channel_id=1, source_target_pairs={{0,8},{4,12},{8,0},{12,4},{16,24},{20,28},{24,16},{28,20},{1,9},{5... | collective-permute-start | bytes 3080 | tf_op jit(solution)/shard_map/ppermute | solution.py:13
  27.4 1.2 %collective-permute-start.2 = (bf16[1024]{0:T(1024)(128)(2,1)S(1)}, bf16[1024]{0:T(1024)(128)(2,1)S(1)}, u32[]{:S(2)}, u32[]{:S(2)}) collective-permute-start(bf16[1024]{0:T(1024)(128)(2,1)S(1)} %maximum_select_fusion.1), channel_id=1, source_target_pairs={{0,16},{4,20},{8,24},{12,28},{16,0},{20,4},{24,8},{28,12},{1,17},{... | collective-permute-start | bytes 6152 | tf_op jit(solution)/shard_map/ppermute | solution.py:13
Sparse Core Ops, SparseCore 0:
  13.7 22.5 all-gather.2
  37.9 21.0 all-gather.4
